TPU v7x, 128 devices: a whole 4x4x4 slice. The times are simulated.
128 devices in a mesh: prow: 8 (over z_hi, y), pcol: 16 (over x, z_lo, core).
Axes of the slice: x: 4, y: 4, z: 4 (z_hi: 2, z_lo: 2; z = z_hi * 2 + z_lo), core: 2. Of those that a mesh axis runs over, the one named last changes fastest.
Arguments:
- panel_t: float32 [16, 256, 8192], P('pcol', None, 'prow'), may hold values from -0.0625 to 0.0625
- ancestor: float32 [8192, 8192], P('prow', 'pcol'), as said below
- structure: int32 [16, 32], replicated, may hold values 0 or 1
- diag_inv: float32 [16, 256, 256], P('pcol'), may hold values from -6 to 6
Outputs:
- inverse_panel: float32 [4096, 8192], P('pcol', 'prow')
- inverse_diag: float32 [16, 256, 256], P('pcol')
Inputs may be any that keep to these rules, and one draw needn't show every extreme that they name: ancestor is symmetric up to rounding.
All inputs are finite; a program needn't handle non-finite values.
Results may differ from a plain program's by a relative error of at most 0.00007.
Values sent between devices are 32-bit elements; how exact they have to be, the bound alone decides.
No kernel may reach another device: no remote copies, remote signals or barrier semaphores. Data moves between devices by JAX's collectives and lax.ppermute only.
A program may use at most 128 MiB of HBM per device.

v0:
```python
import jax
import jax.numpy as jnp
from jax import lax
from jax.experimental import pallas as pl
from jax.experimental.pallas import tpu as pltpu
from jax.sharding import PartitionSpec as P


AXES = ("prow", "pcol")
TILE = 256


def number(x, y, z, core):
    return ((z >> 1) * 4 + y) * 16 + x * 4 + (z & 1) * 2 + core


def pairs(on=None, off=None):
    found = []
    for x in range(4):
        for y in range(4):
            for z in range(4):
                move = on if (y & 1) == (z & 1) else off
                if move is not None:
                    for core in range(2):
                        tx, ty, tz, tc = move(x, y, z, core)
                        found.append((number(x, y, z, core), number(tx % 4, ty % 4, tz % 4, tc)))
    return found


def shift(dy, dz):
    return lambda x, y, z, c: (x, y + (1 - 2 * c) * dy, z + (1 - 2 * c) * dz, c)


def both(move):
    return pairs(move, move)


X_UP = both(lambda x, y, z, c: (x + 1 - 2 * c, y, z, c))
X_DOWN = both(lambda x, y, z, c: (x - 1 + 2 * c, y, z, c))
CORE = both(lambda x, y, z, c: (x, y, z, 1 - c))
Y_BY = [None] + [both(shift(d, 0)) for d in (1, 2, 3)]
Z_FLIP = [None] + [both(lambda x, y, z, c, d=d: (x, y, z ^ d, c)) for d in (1, 2, 3)]


def send(array, route):
    return lax.ppermute(array, AXES, route)


def parts(value):
    high = value.astype(jnp.bfloat16)
    return high, (value - high.astype(jnp.float32)).astype(jnp.bfloat16)


def dot(a, b):
    return lax.dot_general(a, b, (((1,), (1,)), ((), ())), preferred_element_type=jnp.float32)


SLOTS = [
    ((0, -1), (-1, 2)),
    ((0, 1), (1, 2)),
    ((2, -1), (1, -1)),
    ((2, 1), (1, 1)),
    ((0, 0), (-1, 0)),
    ((2, 0), (1, 0)),
    ((0, 2), (-1, -1)),
    ((2, 2), (-1, 1)),
]


def slot_place(where, entry):
    x, y, z, core = where[0], where[1], where[2], where[3]
    on = (y & 1) == (z & 1)
    sign = 1 - 2 * core
    ys = (y + sign * jnp.where(on, entry[0][0], entry[1][0])) & 3
    zs = (z + sign * jnp.where(on, entry[0][1], entry[1][1])) & 3
    delta = (sign * ((((zs >> 1) * 4 + ys) >> 1) - x)) & 3
    place = jnp.where(delta == 0, 0, jnp.where(delta == 3, 1, delta + 1))
    return place * 2 + ((zs ^ z) & 1)


def multiply_kernel(where, structure, *refs):
    own, from_left, f_top, f_bottom, from_right, two_off, t0, w_top, w_bottom, t1, s0, s1, s2, s3 = refs[:14]
    pieces = refs[14:24]
    own_out, mate_top, mate_bottom, *cuts = refs[24:31]
    stage, high, low, result, panel, sems = refs[31:]
    rows, span = own.shape
    half = span // 2
    blocks = span // rows
    step = pl.program_id(0)
    x, y, z, core = where[0], where[1], where[2], where[3]
    on = (y & 1) == (z & 1)
    sign = 1 - 2 * core

    def copies(sources, at):
        height = rows // len(sources)
        for n, source in enumerate(sources):
            part = stage.at[at, pl.ds(n * height, height)]
            pltpu.make_async_copy(source, part, sems.at[at]).start()

    def arrived(at):
        pltpu.make_async_copy(stage.at[at], stage.at[at], sems.at[at]).wait()

    @pl.when(step == 0)
    def _():
        plain = [[ref] for ref in (s0, s1, s2, s3)]
        here = plain + [[own], [f_top, f_bottom], [two_off], [w_top, w_bottom]]
        there = plain + [[from_left], [from_right], [t0], [t1]]
        for a, b, entry in zip(here, there, SLOTS):
            at = slot_place(where, entry)
            if a is b:
                copies(a, at)
            else:
                pl.when(on)(lambda a=a, at=at: copies(a, at))
                pl.when(jnp.logical_not(on))(lambda b=b, at=at: copies(b, at))
        copies([own], 8)
        pl.when((z & 1) != core)(lambda: copies([s0], 9))
        pl.when((z & 1) == core)(lambda: copies([s1], 9))

    def cut_stage(j):
        block = ((x + sign * (0, -1, 1, 2)[j]) & 3) * 2 + (z & 1)
        for side in range(2):
            at = 2 * j + side
            arrived(at)
            supernode = x * 4 + ((z & 1) ^ side) * 2 + core
            for b in range(blocks):
                keep = structure[supernode, block * blocks + b].astype(jnp.float32)
                hi, lo = parts(stage[at, :, b * rows : (b + 1) * rows] * keep)
                g, inner = divmod(b * rows, half)
                row = slice(side * rows, (side + 1) * rows)
                high[2 * j + (g ^ core), row, inner : inner + rows] = hi
                low[2 * j + (g ^ core), row, inner : inner + rows] = lo

    first = step < pl.num_programs(0) // 2
    acc = jnp.zeros((2 * rows, TILE), jnp.float32)

    @pl.when(step == 0)
    def _():
        for j in range(4):
            cut_stage(j)

    for j in range(4):
        for k in range(2):
            if j < 3:
                value = pieces[2 * j + k][...]
            else:
                value = jnp.where(first, pieces[6 + 2 * k][...], pieces[7 + 2 * k][...])
            a, b = parts(value)
            acc += dot(high[2 * j + k], a) + dot(high[2 * j + k], b) + dot(low[2 * j + k], a)
    own_out[...] = acc[:rows]
    mate_top[...] = acc[rows : rows + mate_top.shape[0]]
    mate_bottom[...] = acc[rows + mate_top.shape[0] :]
    hi, lo = parts(acc)
    for side in range(2):
        result[step, side, :rows] = hi[side * rows : (side + 1) * rows]
        result[step, side, rows:] = lo[side * rows : (side + 1) * rows]

    @pl.when(step == 1)
    def _():
        block = (z >> 1) * 4 + y
        for side in range(2):
            arrived(8 + side)
            supernode = x * 4 + ((z & 1) ^ side) * 2 + core
            for b in range(blocks):
                c = slice(b * rows, (b + 1) * rows)
                keep = structure[supernode, block * blocks + b].astype(jnp.float32)
                panel[side, 0, :, c], panel[side, 1, :, c] = parts(stage[8 + side, :, c] * keep)

    @pl.when(step == pl.num_programs(0) - 1)
    def _():
        sums = []
        for side in range(2):
            sum_side = None
            for i in range(blocks):
                c = slice(i * rows, (i + 1) * rows)
                two = dot(result[i, side], panel[side, 0, :, c])
                term = two[:rows] + two[rows:] + dot(result[i, side, :rows], panel[side, 1, :, c])
                sum_side = term if sum_side is None else sum_side + term
            sums.append(sum_side)
        total = sums[0] + jnp.where(on, 0.0, sums[0].T)
        stage[0, :, :rows] = total
        stage[1, :, :rows] = jnp.where(on, sums[1], 0.0)
        quarter = rows // 4
        for d, ref in enumerate(cuts):
            at = pl.multiple_of(((y + sign * d) & 3) * quarter, quarter)
            for side in range(2):
                ref[side] = stage[side, pl.ds(at, quarter), :rows]


def multiply(where, structure, slots, pieces):
    rows, span = slots[0].shape
    half = span // 2
    middle = span // TILE // 2
    at_column = lambda height: pl.BlockSpec((height, TILE), lambda i, *_: (0, i))
    whole = lambda shape: pl.BlockSpec(shape, lambda i, *_: (0,) * len(shape))
    every = pl.BlockSpec((TILE, half), lambda i, *_: (i, 0))
    top = pl.BlockSpec((TILE, half), lambda i, *_: (jnp.minimum(i, middle - 1), 0))
    bottom = pl.BlockSpec((TILE, half), lambda i, *_: (jnp.maximum(i - middle, 0), 0))
    outs = [(rows, span), (rows * 5 // 8, span), (rows * 3 // 8, span)] + [(2, rows // 4, rows)] * 4
    return pl.pallas_call(
        multiply_kernel,
        grid_spec=pltpu.PrefetchScalarGridSpec(
            num_scalar_prefetch=2,
            grid=(span // TILE,),
            in_specs=[pl.BlockSpec(memory_space=pltpu.HBM)] * len(slots) + [every] * 6 + [top, bottom] * 2,
            out_specs=[at_column(shape[0]) for shape in outs[:3]] + [whole(shape) for shape in outs[3:]],
            scratch_shapes=[pltpu.VMEM((10, rows, span), jnp.float32)]
            + [pltpu.VMEM((8, 2 * rows, half), jnp.bfloat16)] * 2
            + [pltpu.VMEM((span // TILE, 2, 2 * rows, TILE), jnp.bfloat16)]
            + [pltpu.VMEM((2, 2, rows, span), jnp.bfloat16), pltpu.SemaphoreType.DMA((10,))],
        ),
        out_shape=[jax.ShapeDtypeStruct(shape, jnp.float32) for shape in outs],
        compiler_params=pltpu.CompilerParams(vmem_limit_bytes=56 * 2**20),
        cost_estimate=pl.CostEstimate(
            flops=48 * rows * span * span, bytes_accessed=4 * (rows * span * 16 + 4 * span * span), transcendentals=0
        ),
    )(where, structure, *slots, *pieces)


def local(panel_t, ancestor, structure, diag_inv):
    width = panel_t.shape[1]
    span = panel_t.shape[2]
    prow = lax.axis_index("prow")
    pcol = lax.axis_index("pcol")
    x = pcol >> 2
    y = prow & 3
    z = (prow >> 2) * 2 + ((pcol >> 1) & 1)
    core = pcol & 1
    on = (y & 1) == (z & 1)
    own = panel_t.reshape(width, span)
    split = width // 2
    half = ancestor.shape[0] // 2

    from_left = send(own, both(shift(1, 0)))
    from_right = send(own, both(shift(-1, 0)))
    two_off = send(own, pairs(on=shift(0, 2)))
    f_top = send(from_left[:split], both(shift(1, 0)))
    lower = from_right[split:]
    f_bottom = send(lower, both(shift(-1, 0)))
    turned = jnp.where(on, two_off, own)
    s0 = send(turned, pairs(on=shift(1, 0), off=shift(0, 1)))
    s1 = send(turned, pairs(on=shift(-1, 0), off=shift(0, -1)))
    t0 = send(from_left, pairs(on=shift(0, 1)))
    t1 = send(from_left, pairs(on=shift(0, -1)))
    crossed = jnp.where(on, from_right, jnp.concatenate([f_top, f_bottom], axis=0))
    s2 = send(crossed, pairs(on=shift(0, 1), off=shift(0, 1)))
    s3 = send(crossed, pairs(on=shift(0, -1), off=shift(0, -1)))
    w_top = send(s0[:split], pairs(off=shift(1, 0)))
    w_bottom = send(s1[split:], pairs(off=shift(-1, 0)))

    left = send(ancestor, X_UP)
    right = send(ancestor, X_DOWN)
    far = [send(left[:half], X_UP), send(right[half:], X_DOWN)]
    pieces = [ancestor, send(ancestor, CORE)]
    pieces += [left, send(right, CORE), right, send(left, CORE)]
    pieces += far + [send(piece, CORE) for piece in far]

    where = jnp.stack([x, y, z, core]).astype(jnp.int32)
    slots = [own, from_left, f_top, f_bottom, from_right, two_off, t0, w_top, w_bottom, t1, s0, s1, s2, s3]
    own_out, mate_top, mate_bottom, *cuts = multiply(where, structure, slots, pieces)
    received = jnp.concatenate([send(mate_top, Z_FLIP[1]), send(mate_bottom, Z_FLIP[1])], axis=0)

    quarter = width // 4
    summed = cuts[0]
    for d in (1, 2, 3):
        summed = summed + send(cuts[d], Y_BY[d])
    mine, mates = summed[0], summed[1]
    total = mine + send(mates, Z_FLIP[1]) + send(mine, Z_FLIP[2]) + send(mates, Z_FLIP[3])
    own_out, total = lax.optimization_barrier((own_out, total))
    diag = jnp.zeros((4, quarter, width), jnp.float32)
    diag = lax.dynamic_update_index_in_dim(diag, total, y, 0)
    for d in (1, 2, 3):
        diag = lax.dynamic_update_index_in_dim(diag, send(total, Y_BY[d]), (y - (1 - 2 * core) * d) & 3, 0)
    return -(own_out + received), diag_inv + diag.reshape(1, width, width)


def solution(mesh):
    return jax.shard_map(
        local,
        mesh=mesh,
        in_specs=(P("pcol", None, "prow"), P("prow", "pcol"), P(), P("pcol", None, None)),
        out_specs=(P("pcol", "prow"), P("pcol", None, None)),
        check_vma=False,
    )
```

profile of v0, /device:TPU:32, one launch (start us, length us, event | category | flops | bytes accessed | tf_op | source)
XLA Modules:
  0.0 191.8 jit_solution(2664698529163109943)
XLA Ops:
  0.6 1.6 collective-permute-start
  3.0 1.6 collective-permute-start.14
  4.6 5.8 %collective-permute-start.2 = (f32[256,1024]{1,0:T(8,128)}, f32[256,1024]{1,0:T(8,128)S(1)}, u32[]{:S(2)}, u32[]{:S(2)}) collective-permute-start(f32[256,1024]{1,0:T(8,128)} %bitcast.26), channel_id=1, source_target_pairs={{0,48},{1,17},{2,50},{3,19},{64,112},{65,81},{66,114},{67,83},{16,... | collective-permute-start | bytes 3145736 | tf_op jit(solution)/shard_map/ppermute | solution.py:46
  10.4 1.7 collective-permute-start.15
  12.1 9.5 %collective-permute-done.refs_1_ = f32[256,1024]{1,0:T(8,128)S(1)} collective-permute-done((f32[256,1024]{1,0:T(8,128)}, f32[256,1024]{1,0:T(8,128)S(1)}, u32[]{:S(2)}, u32[]{:S(2)}) %collective-permute-start) | collective-permute-done | bytes 1048608 | tf_op jit(solution)/shard_map/ppermute | solution.py:46
  23.9 1.7 broadcast_select_fusion
  25.7 9.9 %collective-permute-start.6 = (f32[256,1024]{1,0:T(8,128)S(1)}, f32[256,1024]{1,0:T(8,128)S(1)}, u32[]{:S(2)}, u32[]{:S(2)}) collective-permute-start(f32[256,1024]{1,0:T(8,128)S(1)} %broadcast_select_fusion), channel_id=1, source_target_pairs={{0,16},{1,49},{2,64},{3,1},{64,80},{65,113},{66,0},{67,65},{16,18}... | collective-permute-start | bytes 3145736 | tf_op jit(solution)/shard_map/ppermute | solution.py:46
  35.9 12.4 %collective-permute-done.3.refs_3_ = f32[128,1024]{1,0:T(8,128)S(1)} collective-permute-done((f32[128,1024]{1,0:T(8,128)S(1)}, f32[128,1024]{1,0:T(8,128)S(1)}, u32[]{:S(2)}, u32[]{:S(2)}) %collective-permute-start.3) | collective-permute-done | bytes 524320 | tf_op jit(solution)/shard_map/ppermute | solution.py:46
  48.3 1.8 collective-permute-start.8
  50.1 2.8 %collective-permute-done.6.refs_10_ = f32[256,1024]{1,0:T(8,128)S(1)} collective-permute-done((f32[256,1024]{1,0:T(8,128)S(1)}, f32[256,1024]{1,0:T(8,128)S(1)}, u32[]{:S(2)}, u32[]{:S(2)}) %collective-permute-start.6) | collective-permute-done | bytes 1048608 | tf_op jit(solution)/shard_map/ppermute | solution.py:46
  55.7 4.3 %collective-permute-start.11 = (f32[256,1024]{1,0:T(8,128)S(1)}, f32[256,1024]{1,0:T(8,128)S(1)}, u32[]{:S(2)}, u32[]{:S(2)}) collective-permute-start(f32[256,1024]{1,0:T(8,128)S(1)} %maximum_select_fusion), channel_id=1, source_target_pairs={{0,2},{1,67},{2,64},{3,1},{64,66},{65,3},{66,0},{67,65},{16,18},{1... | collective-permute-start | bytes 3145736 | tf_op jit(solution)/shard_map/ppermute | solution.py:46
  62.6 4.1 %collective-permute-done.8.refs_11_ = f32[256,1024]{1,0:T(8,128)S(1)} collective-permute-done((f32[256,1024]{1,0:T(8,128)S(1)}, f32[256,1024]{1,0:T(8,128)S(1)}, u32[]{:S(2)}, u32[]{:S(2)}) %collective-permute-start.8) | collective-permute-done | bytes 1048608 | tf_op jit(solution)/shard_map/ppermute | solution.py:46
  66.7 2.5 %collective-permute-start.12 = (f32[256,1024]{1,0:T(8,128)S(1)}, f32[256,1024]{1,0:T(8,128)S(1)}, u32[]{:S(2)}, u32[]{:S(2)}) collective-permute-start(f32[256,1024]{1,0:T(8,128)S(1)} %maximum_select_fusion), channel_id=1, source_target_pairs={{0,66},{1,3},{2,0},{3,65},{64,2},{65,67},{66,64},{67,1},{16,82},{1... | collective-permute-start | bytes 3145736 | tf_op jit(solution)/shard_map/ppermute | solution.py:46
  69.2 12.0 %collective-permute-done.10.refs_9_ = f32[256,1024]{1,0:T(8,128)S(1)} collective-permute-done((f32[256,1024]{1,0:T(8,128)S(1)}, f32[256,1024]{1,0:T(8,128)S(1)}, u32[]{:S(2)}, u32[]{:S(2)}) %collective-permute-start.10) | collective-permute-done | bytes 1048608 | tf_op jit(solution)/shard_map/ppermute | solution.py:46
  81.2 2.3 %collective-permute-start.18 = (f32[512,512]{1,0:T(8,128)S(1)}, f32[512,512]{1,0:T(8,128)}, u32[]{:S(2)}, u32[]{:S(2)}) collective-permute-start(f32[512,512]{1,0:T(8,128)S(1)} %slice.36), channel_id=1, source_target_pairs={{0,4},{1,13},{2,6},{3,15},{64,68},{65,77},{66,70},{67,79},{16,20},... | collective-permute-start | bytes 3145736 | tf_op jit(solution)/shard_map/ppermute | solution.py:46
  84.3 3.6 %collective-permute-start.19 = (f32[512,512]{1,0:T(8,128)S(1)}, f32[512,512]{1,0:T(8,128)}, u32[]{:S(2)}, u32[]{:S(2)}) collective-permute-start(f32[512,512]{1,0:T(8,128)S(1)} %slice.37), channel_id=1, source_target_pairs={{0,12},{1,5},{2,14},{3,7},{64,76},{65,69},{66,78},{67,71},{16,28},... | collective-permute-start | bytes 3145736 | tf_op jit(solution)/shard_map/ppermute | solution.py:46
  87.9 13.1 %collective-permute-done.11.refs_12_ = f32[256,1024]{1,0:T(8,128)S(1)} collective-permute-done((f32[256,1024]{1,0:T(8,128)S(1)}, f32[256,1024]{1,0:T(8,128)S(1)}, u32[]{:S(2)}, u32[]{:S(2)}) %collective-permute-start.11) | collective-permute-done | bytes 1048608 | tf_op jit(solution)/shard_map/ppermute | solution.py:46
  103.6 1.3 collective-permute-done.18.refs_20_
  106.0 4.2 %collective-permute-done.7.refs_7_ = f32[128,1024]{1,0:T(8,128)S(1)} collective-permute-done((f32[128,1024]{1,0:T(8,128)S(1)}, f32[128,1024]{1,0:T(8,128)S(1)}, u32[]{:S(2)}, u32[]{:S(2)}) %collective-permute-start.7) | collective-permute-done | bytes 524320 | tf_op jit(solution)/shard_map/ppermute | solution.py:46
  110.3 7.2 %collective-permute-start.9 = (f32[128,1024]{1,0:T(8,128)S(1)}, f32[128,1024]{1,0:T(8,128)}, u32[]{:S(2)}, u32[]{:S(2)}) collective-permute-start(f32[128,1024]{1,0:T(8,128)S(1)} %slice.35), channel_id=1, source_target_pairs={{2,50},{3,19},{66,114},{67,83},{16,0},{17,33},{80,64},{81,97},{34,... | collective-permute-start | bytes 1572872 | tf_op jit(solution)/shard_map/ppermute | solution.py:46
  118.2 5.2 %collective-permute-done.9.refs_8_ = f32[128,1024]{1,0:T(8,128)} collective-permute-done((f32[128,1024]{1,0:T(8,128)S(1)}, f32[128,1024]{1,0:T(8,128)}, u32[]{:S(2)}, u32[]{:S(2)}) %collective-permute-start.9) | collective-permute-done | bytes 524320 | tf_op jit(solution)/shard_map/ppermute | solution.py:46
  124.7 24.8 %shard_map.59 = (f32[256,1024]{1,0:T(8,128)}, f32[160,1024]{1,0:T(8,128)}, f32[96,1024]{1,0:T(8,128)}, f32[2,64,256]{2,1,0:T(8,128)}, f32[2,64,256]{2,1,0:T(8,12...) custom-call(s32[4]{0:T(128)} %pad_add_fusion.where, s32[16,32]{1,0:T(8,128)} %structure.1, f32[256,1024]{1,0:T(8,128)} %bitcast.27, ...), custom_call_target="tpu_custom_call" | custom-call | flops 12884901888 | bytes 33554432 | tf_op jit(solution)/shard_map/pallas_call | solution.py:199
  150.3 4.4 %collective-permute-start.23 = (f32[2,64,256]{2,1,0:T(8,128)}, f32[2,64,256]{2,1,0:T(8,128)S(1)}, u32[]{:S(2)}, u32[]{:S(2)}) collective-permute-start(f32[2,64,256]{2,1,0:T(8,128)} %get-tuple-element.14), channel_id=1, source_target_pairs={{0,32},{1,33},{2,34},{3,35},{64,96},{65,97},{66,98},{67,99},{16,48... | collective-permute-start | bytes 393224 | tf_op jit(solution)/shard_map/ppermute | solution.py:46
  154.8 4.0 %collective-permute-done.22 = f32[2,64,256]{2,1,0:T(8,128)S(1)} collective-permute-done((f32[2,64,256]{2,1,0:T(8,128)}, f32[2,64,256]{2,1,0:T(8,128)S(1)}, u32[]{:S(2)}, u32[]{:S(2)}) %collective-permute-start.22) | collective-permute-done | bytes 131104 | tf_op jit(solution)/shard_map/ppermute | solution.py:46
  158.8 2.7 %collective-permute-done.23 = f32[2,64,256]{2,1,0:T(8,128)S(1)} collective-permute-done((f32[2,64,256]{2,1,0:T(8,128)}, f32[2,64,256]{2,1,0:T(8,128)S(1)}, u32[]{:S(2)}, u32[]{:S(2)}) %collective-permute-start.23) | collective-permute-done | bytes 131104 | tf_op jit(solution)/shard_map/ppermute | solution.py:46
  162.7 2.9 %collective-permute-start.26 = (f32[64,256]{1,0:T(8,128)S(1)}, f32[64,256]{1,0:T(8,128)S(1)}, u32[]{:S(2)}, u32[]{:S(2)}) collective-permute-start(f32[64,256]{1,0:T(8,128)S(1)} %get-tuple-element.20), channel_id=1, source_target_pairs={{0,64},{1,65},{2,66},{3,67},{64,0},{65,1},{66,2},{67,3},{16,80},{1... | collective-permute-start | bytes 196616 | tf_op jit(solution)/shard_map/ppermute | solution.py:46
  166.1 2.1 %collective-permute-start.28 = (f32[160,1024]{1,0:T(8,128)}, f32[160,1024]{1,0:T(8,128)S(1)}, u32[]{:S(2)}, u32[]{:S(2)}) collective-permute-start(f32[160,1024]{1,0:T(8,128)} %get-tuple-element.17), channel_id=1, source_target_pairs={{0,2},{1,3},{2,0},{3,1},{64,66},{65,67},{66,64},{67,65},{16,18},{1... | collective-permute-start | bytes 1966088 | tf_op jit(solution)/shard_map/ppermute | solution.py:46
  168.5 1.4 collective-permute-done.27
  170.2 3.3 %collective-permute-start.31 = (f32[64,256]{1,0:T(8,128)S(1)}, f32[64,256]{1,0:T(8,128)S(1)}, u32[]{:S(2)}, u32[]{:S(2)}) collective-permute-start(f32[64,256]{1,0:T(8,128)S(1)} %add_add_fusion.1), channel_id=1, source_target_pairs={{0,32},{1,33},{2,34},{3,35},{64,96},{65,97},{66,98},{67,99},{16,48... | collective-permute-start | bytes 196616 | tf_op jit(solution)/shard_map/ppermute | solution.py:46
  173.5 1.9 %collective-permute-done.30 = f32[64,256]{1,0:T(8,128)S(1)} collective-permute-done((f32[64,256]{1,0:T(8,128)S(1)}, f32[64,256]{1,0:T(8,128)S(1)}, u32[]{:S(2)}, u32[]{:S(2)}) %collective-permute-start.30) | collective-permute-done | bytes 65568 | tf_op jit(solution)/shard_map/ppermute | solution.py:46
  176.4 1.3 collective-permute-done.32
  178.5 12.2 %collective-permute-done.29 = f32[96,1024]{1,0:T(8,128)S(1)} collective-permute-done((f32[96,1024]{1,0:T(8,128)}, f32[96,1024]{1,0:T(8,128)S(1)}, u32[]{:S(2)}, u32[]{:S(2)}) %collective-permute-start.29) | collective-permute-done | bytes 393248 | tf_op jit(solution)/shard_map/ppermute | solution.py:46
  (90 shorter events, 21.1 us)
Async XLA Ops:
  0.6 21.0 %collective-permute-start = (f32[256,1024]{1,0:T(8,128)}, f32[256,1024]{1,0:T(8,128)S(1)}, u32[]{:S(2)}, u32[]{:S(2)}) collective-permute-start(f32[256,1024]{1,0:T(8,128)} %bitcast.24), channel_id=1, source_target_pairs={{0,16},{1,49},{2,18},{3,51},{64,80},{65,113},{66,82},{67,115},{16,... | collective-permute-start | bytes 3145736 | tf_op jit(solution)/shard_map/ppermute | solution.py:46
  2.3 21.7 %collective-permute-start.4 = (f32[256,1024]{1,0:T(8,128)}, f32[256,1024]{1,0:T(8,128)S(1)}, u32[]{:S(2)}, u32[]{:S(2)}) collective-permute-start(f32[256,1024]{1,0:T(8,128)} %bitcast.25), channel_id=1, source_target_pairs={{0,64},{1,65},{64,0},{65,1},{18,82},{19,83},{82,18},{83,19},{32,96... | collective-permute-start | bytes 3145736 | tf_op jit(solution)/shard_map/ppermute | solution.py:46
  3.0 51.2 %collective-permute-start.14 = (f32[1024,512]{1,0:T(8,128)}, f32[1024,512]{1,0:T(8,128)}, u32[]{:S(2)}, u32[]{:S(2)}) collective-permute-start(f32[1024,512]{1,0:T(8,128)} %refs_14_.1), channel_id=1, source_target_pairs={{0,4},{1,13},{2,6},{3,15},{64,68},{65,77},{66,70},{67,79},{16,20},... | collective-permute-start | bytes 6291464 | tf_op jit(solution)/shard_map/ppermute | solution.py:46
  4.6 31.1 %collective-permute-start.2 = (f32[256,1024]{1,0:T(8,128)}, f32[256,1024]{1,0:T(8,128)S(1)}, u32[]{:S(2)}, u32[]{:S(2)}) collective-permute-start(f32[256,1024]{1,0:T(8,128)} %bitcast.26), channel_id=1, source_target_pairs={{0,48},{1,17},{2,50},{3,19},{64,112},{65,81},{66,114},{67,83},{16,... | collective-permute-start | bytes 3145736 | tf_op jit(solution)/shard_map/ppermute | solution.py:46
  10.4 45.3 %collective-permute-start.15 = (f32[1024,512]{1,0:T(8,128)}, f32[1024,512]{1,0:T(8,128)}, u32[]{:S(2)}, u32[]{:S(2)}) collective-permute-start(f32[1024,512]{1,0:T(8,128)} %refs_14_.1), channel_id=1, source_target_pairs={{0,12},{1,5},{2,14},{3,7},{64,76},{65,69},{66,78},{67,71},{16,28},... | collective-permute-start | bytes 6291464 | tf_op jit(solution)/shard_map/ppermute | solution.py:46
  22.6 13.1 %collective-permute-start.1 = (f32[128,1024]{1,0:T(8,128)S(1)}, f32[128,1024]{1,0:T(8,128)S(1)}, u32[]{:S(2)}, u32[]{:S(2)}) collective-permute-start(f32[128,1024]{1,0:T(8,128)S(1)} %slice.32), channel_id=1, source_target_pairs={{0,16},{1,49},{2,18},{3,51},{64,80},{65,113},{66,82},{67,115},{16,... | collective-permute-start | bytes 1572872 | tf_op jit(solution)/shard_map/ppermute | solution.py:46
  25.7 27.2 %collective-permute-start.6 = (f32[256,1024]{1,0:T(8,128)S(1)}, f32[256,1024]{1,0:T(8,128)S(1)}, u32[]{:S(2)}, u32[]{:S(2)}) collective-permute-start(f32[256,1024]{1,0:T(8,128)S(1)} %broadcast_select_fusion), channel_id=1, source_target_pairs={{0,16},{1,49},{2,64},{3,1},{64,80},{65,113},{66,0},{67,65},{16,18}... | collective-permute-start | bytes 3145736 | tf_op jit(solution)/shard_map/ppermute | solution.py:46
  35.6 52.3 %collective-permute-start.13 = (f32[1024,512]{1,0:T(8,128)S(1)}, f32[1024,512]{1,0:T(8,128)S(1)}, u32[]{:S(2)}, u32[]{:S(2)}) collective-permute-start(f32[1024,512]{1,0:T(8,128)S(1)} %copy-done.10), channel_id=1, source_target_pairs={{0,1},{1,0},{2,3},{3,2},{64,65},{65,64},{66,67},{67,66},{16,17},{1... | collective-permute-start | bytes 6291464 | tf_op jit(solution)/shard_map/ppermute | solution.py:46
  35.8 12.5 %collective-permute-start.3 = (f32[128,1024]{1,0:T(8,128)S(1)}, f32[128,1024]{1,0:T(8,128)S(1)}, u32[]{:S(2)}, u32[]{:S(2)}) collective-permute-start(f32[128,1024]{1,0:T(8,128)S(1)} %slice.33), channel_id=1, source_target_pairs={{0,48},{1,17},{2,50},{3,19},{64,112},{65,81},{66,114},{67,83},{16,... | collective-permute-start | bytes 1572872 | tf_op jit(solution)/shard_map/ppermute | solution.py:46
  48.3 18.4 %collective-permute-start.8 = (f32[256,1024]{1,0:T(8,128)S(1)}, f32[256,1024]{1,0:T(8,128)S(1)}, u32[]{:S(2)}, u32[]{:S(2)}) collective-permute-start(f32[256,1024]{1,0:T(8,128)S(1)} %broadcast_select_fusion), channel_id=1, source_target_pairs={{0,48},{1,17},{2,0},{3,65},{64,112},{65,81},{66,64},{67,1},{16,82}... | collective-permute-start | bytes 3145736 | tf_op jit(solution)/shard_map/ppermute | solution.py:46
  52.9 28.3 %collective-permute-start.10 = (f32[256,1024]{1,0:T(8,128)S(1)}, f32[256,1024]{1,0:T(8,128)S(1)}, u32[]{:S(2)}, u32[]{:S(2)}) collective-permute-start(f32[256,1024]{1,0:T(8,128)S(1)} %copy-done.7), channel_id=1, source_target_pairs={{0,66},{1,3},{64,2},{65,67},{18,16},{19,81},{82,80},{83,17},{32,98... | collective-permute-start | bytes 3145736 | tf_op jit(solution)/shard_map/ppermute | solution.py:46
  54.2 30.1 %collective-permute-start.5 = (f32[256,1024]{1,0:T(8,128)S(1)}, f32[256,1024]{1,0:T(8,128)S(1)}, u32[]{:S(2)}, u32[]{:S(2)}) collective-permute-start(f32[256,1024]{1,0:T(8,128)S(1)} %copy-done.7), channel_id=1, source_target_pairs={{0,2},{1,67},{64,66},{65,3},{18,80},{19,17},{82,16},{83,81},{32,34... | collective-permute-start | bytes 3145736 | tf_op jit(solution)/shard_map/ppermute | solution.py:46
  55.7 45.3 %collective-permute-start.11 = (f32[256,1024]{1,0:T(8,128)S(1)}, f32[256,1024]{1,0:T(8,128)S(1)}, u32[]{:S(2)}, u32[]{:S(2)}) collective-permute-start(f32[256,1024]{1,0:T(8,128)S(1)} %maximum_select_fusion), channel_id=1, source_target_pairs={{0,2},{1,67},{2,64},{3,1},{64,66},{65,3},{66,0},{67,65},{16,18},{1... | collective-permute-start | bytes 3145736 | tf_op jit(solution)/shard_map/ppermute | solution.py:46
  66.7 35.6 %collective-permute-start.12 = (f32[256,1024]{1,0:T(8,128)S(1)}, f32[256,1024]{1,0:T(8,128)S(1)}, u32[]{:S(2)}, u32[]{:S(2)}) collective-permute-start(f32[256,1024]{1,0:T(8,128)S(1)} %maximum_select_fusion), channel_id=1, source_target_pairs={{0,66},{1,3},{2,0},{3,65},{64,2},{65,67},{66,64},{67,1},{16,82},{1... | collective-permute-start | bytes 3145736 | tf_op jit(solution)/shard_map/ppermute | solution.py:46
  81.2 23.7 %collective-permute-start.18 = (f32[512,512]{1,0:T(8,128)S(1)}, f32[512,512]{1,0:T(8,128)}, u32[]{:S(2)}, u32[]{:S(2)}) collective-permute-start(f32[512,512]{1,0:T(8,128)S(1)} %slice.36), channel_id=1, source_target_pairs={{0,4},{1,13},{2,6},{3,15},{64,68},{65,77},{66,70},{67,79},{16,20},... | collective-permute-start | bytes 3145736 | tf_op jit(solution)/shard_map/ppermute | solution.py:46
  84.3 21.6 %collective-permute-start.19 = (f32[512,512]{1,0:T(8,128)S(1)}, f32[512,512]{1,0:T(8,128)}, u32[]{:S(2)}, u32[]{:S(2)}) collective-permute-start(f32[512,512]{1,0:T(8,128)S(1)} %slice.37), channel_id=1, source_target_pairs={{0,12},{1,5},{2,14},{3,7},{64,76},{65,69},{66,78},{67,71},{16,28},... | collective-permute-start | bytes 3145736 | tf_op jit(solution)/shard_map/ppermute | solution.py:46
  87.9 35.5 %collective-permute-start.16 = (f32[1024,512]{1,0:T(8,128)}, f32[1024,512]{1,0:T(8,128)S(1)}, u32[]{:S(2)}, u32[]{:S(2)}) collective-permute-start(f32[1024,512]{1,0:T(8,128)} %collective-permute-done.15.refs_18_), channel_id=1, source_target_pairs={{0,1},{1,0},{2,3},{3,2},{64,65},{65,64},{66,67},{67,66},{16,17},{1... | collective-permute-start | bytes 6291464 | tf_op jit(solution)/shard_map/ppermute | solution.py:46
  101.0 22.4 %collective-permute-start.17 = (f32[1024,512]{1,0:T(8,128)}, f32[1024,512]{1,0:T(8,128)}, u32[]{:S(2)}, u32[]{:S(2)}) collective-permute-start(f32[1024,512]{1,0:T(8,128)} %collective-permute-done.14.refs_16_), channel_id=1, source_target_pairs={{0,1},{1,0},{2,3},{3,2},{64,65},{65,64},{66,67},{67,66},{16,17},{1... | collective-permute-start | bytes 6291464 | tf_op jit(solution)/shard_map/ppermute | solution.py:46
  102.3 8.0 %collective-permute-start.7 = (f32[128,1024]{1,0:T(8,128)S(1)}, f32[128,1024]{1,0:T(8,128)S(1)}, u32[]{:S(2)}, u32[]{:S(2)}) collective-permute-start(f32[128,1024]{1,0:T(8,128)S(1)} %slice.34), channel_id=1, source_target_pairs={{2,18},{3,51},{66,82},{67,115},{16,32},{17,1},{80,96},{81,65},{34,... | collective-permute-start | bytes 1572872 | tf_op jit(solution)/shard_map/ppermute | solution.py:46
  104.9 18.4 %collective-permute-start.20 = (f32[512,512]{1,0:T(8,128)}, f32[512,512]{1,0:T(8,128)}, u32[]{:S(2)}, u32[]{:S(2)}) collective-permute-start(f32[512,512]{1,0:T(8,128)} %collective-permute-done.18.refs_20_), channel_id=1, source_target_pairs={{0,1},{1,0},{2,3},{3,2},{64,65},{65,64},{66,67},{67,66},{16,17},{1... | collective-permute-start | bytes 3145736 | tf_op jit(solution)/shard_map/ppermute | solution.py:46
  105.9 17.5 %collective-permute-start.21 = (f32[512,512]{1,0:T(8,128)}, f32[512,512]{1,0:T(8,128)}, u32[]{:S(2)}, u32[]{:S(2)}) collective-permute-start(f32[512,512]{1,0:T(8,128)} %collective-permute-done.19.refs_21_), channel_id=1, source_target_pairs={{0,1},{1,0},{2,3},{3,2},{64,65},{65,64},{66,67},{67,66},{16,17},{1... | collective-permute-start | bytes 3145736 | tf_op jit(solution)/shard_map/ppermute | solution.py:46
  110.3 13.1 %collective-permute-start.9 = (f32[128,1024]{1,0:T(8,128)S(1)}, f32[128,1024]{1,0:T(8,128)}, u32[]{:S(2)}, u32[]{:S(2)}) collective-permute-start(f32[128,1024]{1,0:T(8,128)S(1)} %slice.35), channel_id=1, source_target_pairs={{2,50},{3,19},{66,114},{67,83},{16,0},{17,33},{80,64},{81,97},{34,... | collective-permute-start | bytes 1572872 | tf_op jit(solution)/shard_map/ppermute | solution.py:46
  149.5 9.2 %collective-permute-start.22 = (f32[2,64,256]{2,1,0:T(8,128)}, f32[2,64,256]{2,1,0:T(8,128)S(1)}, u32[]{:S(2)}, u32[]{:S(2)}) collective-permute-start(f32[2,64,256]{2,1,0:T(8,128)} %get-tuple-element.13), channel_id=1, source_target_pairs={{0,16},{1,49},{2,18},{3,51},{64,80},{65,113},{66,82},{67,115},{16,... | collective-permute-start | bytes 393224 | tf_op jit(solution)/shard_map/ppermute | solution.py:46
  150.3 11.1 %collective-permute-start.23 = (f32[2,64,256]{2,1,0:T(8,128)}, f32[2,64,256]{2,1,0:T(8,128)S(1)}, u32[]{:S(2)}, u32[]{:S(2)}) collective-permute-start(f32[2,64,256]{2,1,0:T(8,128)} %get-tuple-element.14), channel_id=1, source_target_pairs={{0,32},{1,33},{2,34},{3,35},{64,96},{65,97},{66,98},{67,99},{16,48... | collective-permute-start | bytes 393224 | tf_op jit(solution)/shard_map/ppermute | solution.py:46
  154.8 6.7 %collective-permute-start.24 = (f32[2,64,256]{2,1,0:T(8,128)}, f32[2,64,256]{2,1,0:T(8,128)S(1)}, u32[]{:S(2)}, u32[]{:S(2)}) collective-permute-start(f32[2,64,256]{2,1,0:T(8,128)} %get-tuple-element.15), channel_id=1, source_target_pairs={{0,48},{1,17},{2,50},{3,19},{64,112},{65,81},{66,114},{67,83},{16,... | collective-permute-start | bytes 393224 | tf_op jit(solution)/shard_map/ppermute | solution.py:46
  162.4 5.8 %collective-permute-start.25 = (f32[64,256]{1,0:T(8,128)S(1)}, f32[64,256]{1,0:T(8,128)S(1)}, u32[]{:S(2)}, u32[]{:S(2)}) collective-permute-start(f32[64,256]{1,0:T(8,128)S(1)} %get-tuple-element.21), channel_id=1, source_target_pairs={{0,2},{1,3},{2,0},{3,1},{64,66},{65,67},{66,64},{67,65},{16,18},{1... | collective-permute-start | bytes 196616 | tf_op jit(solution)/shard_map/ppermute | solution.py:46
  162.7 5.8 %collective-permute-start.26 = (f32[64,256]{1,0:T(8,128)S(1)}, f32[64,256]{1,0:T(8,128)S(1)}, u32[]{:S(2)}, u32[]{:S(2)}) collective-permute-start(f32[64,256]{1,0:T(8,128)S(1)} %get-tuple-element.20), channel_id=1, source_target_pairs={{0,64},{1,65},{2,66},{3,67},{64,0},{65,1},{66,2},{67,3},{16,80},{1... | collective-permute-start | bytes 196616 | tf_op jit(solution)/shard_map/ppermute | solution.py:46
  166.1 24.6 %collective-permute-start.28 = (f32[160,1024]{1,0:T(8,128)}, f32[160,1024]{1,0:T(8,128)S(1)}, u32[]{:S(2)}, u32[]{:S(2)}) collective-permute-start(f32[160,1024]{1,0:T(8,128)} %get-tuple-element.17), channel_id=1, source_target_pairs={{0,2},{1,3},{2,0},{3,1},{64,66},{65,67},{66,64},{67,65},{16,18},{1... | collective-permute-start | bytes 1966088 | tf_op jit(solution)/shard_map/ppermute | solution.py:46
  168.1 22.5 %collective-permute-start.29 = (f32[96,1024]{1,0:T(8,128)}, f32[96,1024]{1,0:T(8,128)S(1)}, u32[]{:S(2)}, u32[]{:S(2)}) collective-permute-start(f32[96,1024]{1,0:T(8,128)} %get-tuple-element.18), channel_id=1, source_target_pairs={{0,2},{1,3},{2,0},{3,1},{64,66},{65,67},{66,64},{67,65},{16,18},{1... | collective-permute-start | bytes 1179656 | tf_op jit(solution)/shard_map/ppermute | solution.py:46
  169.9 5.5 %collective-permute-start.30 = (f32[64,256]{1,0:T(8,128)S(1)}, f32[64,256]{1,0:T(8,128)S(1)}, u32[]{:S(2)}, u32[]{:S(2)}) collective-permute-start(f32[64,256]{1,0:T(8,128)S(1)} %add_add_fusion.1), channel_id=1, source_target_pairs={{0,16},{1,49},{2,18},{3,51},{64,80},{65,113},{66,82},{67,115},{16,... | collective-permute-start | bytes 196616 | tf_op jit(solution)/shard_map/ppermute | solution.py:46
  170.2 6.2 %collective-permute-start.31 = (f32[64,256]{1,0:T(8,128)S(1)}, f32[64,256]{1,0:T(8,128)S(1)}, u32[]{:S(2)}, u32[]{:S(2)}) collective-permute-start(f32[64,256]{1,0:T(8,128)S(1)} %add_add_fusion.1), channel_id=1, source_target_pairs={{0,32},{1,33},{2,34},{3,35},{64,96},{65,97},{66,98},{67,99},{16,48... | collective-permute-start | bytes 196616 | tf_op jit(solution)/shard_map/ppermute | solution.py:46
  173.5 4.3 %collective-permute-start.32 = (f32[64,256]{1,0:T(8,128)S(1)}, f32[64,256]{1,0:T(8,128)S(1)}, u32[]{:S(2)}, u32[]{:S(2)}) collective-permute-start(f32[64,256]{1,0:T(8,128)S(1)} %add_add_fusion.1), channel_id=1, source_target_pairs={{0,48},{1,17},{2,50},{3,19},{64,112},{65,81},{66,114},{67,83},{16,... | collective-permute-start | bytes 196616 | tf_op jit(solution)/shard_map/ppermute | solution.py:46
  (19 other events, 399.6 us)
where the time goes:
time: 193 us; the launch traced here: 192 us
  waiting for transfers between devices  91.3 us (47%)
  starting transfers between devices  64.2 us (33%)
  Pallas kernels  24.8 us (13%)
  other arithmetic  5.39 us (3%)
  local copies, waits for them, and re-layouts  5.12 us (3%)
    ppermute x33, waiting for transfers between devices, send(): return lax.ppermute(array, AXES, route)  91.3 us
    ppermute x33, starting transfers between devices, send(): return lax.ppermute(array, AXES, route)  64.2 us
    pallas_call x1, Pallas kernels, multiply(): pl.pallas_call(multiply_kernel, grid_spec=pltpu.PrefetchScalarGridSpec(nu...  24.8 us
  transfers between devices with their start and end apart: 33, of which 19 were waited for; matrix products, arithmetic and copies ran while one was open for 3% of the time, Pallas kernels for 0%

commit v1 on v0

--- a/solution.py
+++ b/solution.py
@@ -147,8 +147,8 @@
             a, b = parts(value)
             acc += dot(high[2 * j + k], a) + dot(high[2 * j + k], b) + dot(low[2 * j + k], a)
     own_out[...] = acc[:rows]
-    mate_top[...] = acc[rows : rows + mate_top.shape[0]]
-    mate_bottom[...] = acc[rows + mate_top.shape[0] :]
+    mate_top[...] = acc[rows : rows + rows // 2]
+    mate_bottom[...] = acc[rows + rows // 2 :]
     hi, lo = parts(acc)
     for side in range(2):
         result[step, side, :rows] = hi[side * rows : (side + 1) * rows]
@@ -195,7 +195,7 @@
     every = pl.BlockSpec((TILE, half), lambda i, *_: (i, 0))
     top = pl.BlockSpec((TILE, half), lambda i, *_: (jnp.minimum(i, middle - 1), 0))
     bottom = pl.BlockSpec((TILE, half), lambda i, *_: (jnp.maximum(i - middle, 0), 0))
-    outs = [(rows, span), (rows * 5 // 8, span), (rows * 3 // 8, span)] + [(2, rows // 4, rows)] * 4
+    outs = [(rows, span), (rows // 2, span), (rows // 2, span)] + [(2, rows // 4, rows)] * 4
     return pl.pallas_call(
         multiply_kernel,
         grid_spec=pltpu.PrefetchScalarGridSpec(

time: 193 us -> 193 us (level)
  transfers between devices with their start and end apart: 33 -> 33, of which waited for: 19 -> 20; matrix products, arithmetic and copies ran while one was open for 3% -> 3% of each run, Pallas kernels for 0% -> 0%
where the time goes in v1:
time: 193 us; the launch traced here: 192 us
  waiting for transfers between devices  91.3 us (47%)
  starting transfers between devices  64.2 us (33%)
  Pallas kernels  24.8 us (13%)
  other arithmetic  5.39 us (3%)
  local copies, waits for them, and re-layouts  5.12 us (3%)
    ppermute x33, waiting for transfers between devices, send(): return lax.ppermute(array, AXES, route)  91.3 us
    ppermute x33, starting transfers between devices, send(): return lax.ppermute(array, AXES, route)  64.2 us
    pallas_call x1, Pallas kernels, multiply(): pl.pallas_call(multiply_kernel, grid_spec=pltpu.PrefetchScalarGridSpec(nu...  24.8 us
  transfers between devices with their start and end apart: 33, of which 20 were waited for; matrix products, arithmetic and copies ran while one was open for 3% of the time, Pallas kernels for 0%

profile of v1, /device:TPU:32, one launch (start us, length us, event | category | flops | bytes accessed | tf_op | source)
XLA Modules:
  0.0 191.8 jit_solution(2605638002340528985)
XLA Ops:
  0.6 1.6 collective-permute-start
  3.0 1.6 collective-permute-start.14
  4.6 5.8 %collective-permute-start.2 = (f32[256,1024]{1,0:T(8,128)}, f32[256,1024]{1,0:T(8,128)S(1)}, u32[]{:S(2)}, u32[]{:S(2)}) collective-permute-start(f32[256,1024]{1,0:T(8,128)} %bitcast.26), channel_id=1, source_target_pairs={{0,48},{1,17},{2,50},{3,19},{64,112},{65,81},{66,114},{67,83},{16,... | collective-permute-start | bytes 3145736 | tf_op jit(solution)/shard_map/ppermute | solution.py:46
  10.4 1.7 collective-permute-start.15
  12.1 9.5 %collective-permute-done.refs_1_ = f32[256,1024]{1,0:T(8,128)S(1)} collective-permute-done((f32[256,1024]{1,0:T(8,128)}, f32[256,1024]{1,0:T(8,128)S(1)}, u32[]{:S(2)}, u32[]{:S(2)}) %collective-permute-start) | collective-permute-done | bytes 1048608 | tf_op jit(solution)/shard_map/ppermute | solution.py:46
  23.9 1.7 broadcast_select_fusion
  25.7 9.9 %collective-permute-start.6 = (f32[256,1024]{1,0:T(8,128)S(1)}, f32[256,1024]{1,0:T(8,128)S(1)}, u32[]{:S(2)}, u32[]{:S(2)}) collective-permute-start(f32[256,1024]{1,0:T(8,128)S(1)} %broadcast_select_fusion), channel_id=1, source_target_pairs={{0,16},{1,49},{2,64},{3,1},{64,80},{65,113},{66,0},{67,65},{16,18}... | collective-permute-start | bytes 3145736 | tf_op jit(solution)/shard_map/ppermute | solution.py:46
  35.9 12.4 %collective-permute-done.3.refs_3_ = f32[128,1024]{1,0:T(8,128)S(1)} collective-permute-done((f32[128,1024]{1,0:T(8,128)S(1)}, f32[128,1024]{1,0:T(8,128)S(1)}, u32[]{:S(2)}, u32[]{:S(2)}) %collective-permute-start.3) | collective-permute-done | bytes 524320 | tf_op jit(solution)/shard_map/ppermute | solution.py:46
  48.3 1.8 collective-permute-start.8
  50.1 2.8 %collective-permute-done.6.refs_10_ = f32[256,1024]{1,0:T(8,128)S(1)} collective-permute-done((f32[256,1024]{1,0:T(8,128)S(1)}, f32[256,1024]{1,0:T(8,128)S(1)}, u32[]{:S(2)}, u32[]{:S(2)}) %collective-permute-start.6) | collective-permute-done | bytes 1048608 | tf_op jit(solution)/shard_map/ppermute | solution.py:46
  55.7 4.3 %collective-permute-start.11 = (f32[256,1024]{1,0:T(8,128)S(1)}, f32[256,1024]{1,0:T(8,128)S(1)}, u32[]{:S(2)}, u32[]{:S(2)}) collective-permute-start(f32[256,1024]{1,0:T(8,128)S(1)} %maximum_select_fusion), channel_id=1, source_target_pairs={{0,2},{1,67},{2,64},{3,1},{64,66},{65,3},{66,0},{67,65},{16,18},{1... | collective-permute-start | bytes 3145736 | tf_op jit(solution)/shard_map/ppermute | solution.py:46
  62.6 4.1 %collective-permute-done.8.refs_11_ = f32[256,1024]{1,0:T(8,128)S(1)} collective-permute-done((f32[256,1024]{1,0:T(8,128)S(1)}, f32[256,1024]{1,0:T(8,128)S(1)}, u32[]{:S(2)}, u32[]{:S(2)}) %collective-permute-start.8) | collective-permute-done | bytes 1048608 | tf_op jit(solution)/shard_map/ppermute | solution.py:46
  66.7 2.5 %collective-permute-start.12 = (f32[256,1024]{1,0:T(8,128)S(1)}, f32[256,1024]{1,0:T(8,128)S(1)}, u32[]{:S(2)}, u32[]{:S(2)}) collective-permute-start(f32[256,1024]{1,0:T(8,128)S(1)} %maximum_select_fusion), channel_id=1, source_target_pairs={{0,66},{1,3},{2,0},{3,65},{64,2},{65,67},{66,64},{67,1},{16,82},{1... | collective-permute-start | bytes 3145736 | tf_op jit(solution)/shard_map/ppermute | solution.py:46
  69.2 12.0 %collective-permute-done.10.refs_9_ = f32[256,1024]{1,0:T(8,128)S(1)} collective-permute-done((f32[256,1024]{1,0:T(8,128)S(1)}, f32[256,1024]{1,0:T(8,128)S(1)}, u32[]{:S(2)}, u32[]{:S(2)}) %collective-permute-start.10) | collective-permute-done | bytes 1048608 | tf_op jit(solution)/shard_map/ppermute | solution.py:46
  81.2 2.3 %collective-permute-start.18 = (f32[512,512]{1,0:T(8,128)S(1)}, f32[512,512]{1,0:T(8,128)}, u32[]{:S(2)}, u32[]{:S(2)}) collective-permute-start(f32[512,512]{1,0:T(8,128)S(1)} %slice.36), channel_id=1, source_target_pairs={{0,4},{1,13},{2,6},{3,15},{64,68},{65,77},{66,70},{67,79},{16,20},... | collective-permute-start | bytes 3145736 | tf_op jit(solution)/shard_map/ppermute | solution.py:46
  84.3 3.6 %collective-permute-start.19 = (f32[512,512]{1,0:T(8,128)S(1)}, f32[512,512]{1,0:T(8,128)}, u32[]{:S(2)}, u32[]{:S(2)}) collective-permute-start(f32[512,512]{1,0:T(8,128)S(1)} %slice.37), channel_id=1, source_target_pairs={{0,12},{1,5},{2,14},{3,7},{64,76},{65,69},{66,78},{67,71},{16,28},... | collective-permute-start | bytes 3145736 | tf_op jit(solution)/shard_map/ppermute | solution.py:46
  87.9 13.1 %collective-permute-done.11.refs_12_ = f32[256,1024]{1,0:T(8,128)S(1)} collective-permute-done((f32[256,1024]{1,0:T(8,128)S(1)}, f32[256,1024]{1,0:T(8,128)S(1)}, u32[]{:S(2)}, u32[]{:S(2)}) %collective-permute-start.11) | collective-permute-done | bytes 1048608 | tf_op jit(solution)/shard_map/ppermute | solution.py:46
  103.6 1.3 collective-permute-done.18.refs_20_
  106.0 4.2 %collective-permute-done.7.refs_7_ = f32[128,1024]{1,0:T(8,128)S(1)} collective-permute-done((f32[128,1024]{1,0:T(8,128)S(1)}, f32[128,1024]{1,0:T(8,128)S(1)}, u32[]{:S(2)}, u32[]{:S(2)}) %collective-permute-start.7) | collective-permute-done | bytes 524320 | tf_op jit(solution)/shard_map/ppermute | solution.py:46
  110.3 7.2 %collective-permute-start.9 = (f32[128,1024]{1,0:T(8,128)S(1)}, f32[128,1024]{1,0:T(8,128)}, u32[]{:S(2)}, u32[]{:S(2)}) collective-permute-start(f32[128,1024]{1,0:T(8,128)S(1)} %slice.35), channel_id=1, source_target_pairs={{2,50},{3,19},{66,114},{67,83},{16,0},{17,33},{80,64},{81,97},{34,... | collective-permute-start | bytes 1572872 | tf_op jit(solution)/shard_map/ppermute | solution.py:46
  118.1 5.2 %collective-permute-done.9.refs_8_ = f32[128,1024]{1,0:T(8,128)} collective-permute-done((f32[128,1024]{1,0:T(8,128)S(1)}, f32[128,1024]{1,0:T(8,128)}, u32[]{:S(2)}, u32[]{:S(2)}) %collective-permute-start.9) | collective-permute-done | bytes 524320 | tf_op jit(solution)/shard_map/ppermute | solution.py:46
  124.7 24.8 %shard_map.59 = (f32[256,1024]{1,0:T(8,128)}, f32[128,1024]{1,0:T(8,128)}, f32[128,1024]{1,0:T(8,128)}, f32[2,64,256]{2,1,0:T(8,128)}, f32[2,64,256]{2,1,0:T(8,1...) custom-call(s32[4]{0:T(128)} %pad_add_fusion.where, s32[16,32]{1,0:T(8,128)} %structure.1, f32[256,1024]{1,0:T(8,128)} %bitcast.27, ...), custom_call_target="tpu_custom_call" | custom-call | flops 12884901888 | bytes 33554432 | tf_op jit(solution)/shard_map/pallas_call | solution.py:199
  150.3 4.4 %collective-permute-start.23 = (f32[2,64,256]{2,1,0:T(8,128)}, f32[2,64,256]{2,1,0:T(8,128)S(1)}, u32[]{:S(2)}, u32[]{:S(2)}) collective-permute-start(f32[2,64,256]{2,1,0:T(8,128)} %get-tuple-element.14), channel_id=1, source_target_pairs={{0,32},{1,33},{2,34},{3,35},{64,96},{65,97},{66,98},{67,99},{16,48... | collective-permute-start | bytes 393224 | tf_op jit(solution)/shard_map/ppermute | solution.py:46
  154.8 4.0 %collective-permute-done.22 = f32[2,64,256]{2,1,0:T(8,128)S(1)} collective-permute-done((f32[2,64,256]{2,1,0:T(8,128)}, f32[2,64,256]{2,1,0:T(8,128)S(1)}, u32[]{:S(2)}, u32[]{:S(2)}) %collective-permute-start.22) | collective-permute-done | bytes 131104 | tf_op jit(solution)/shard_map/ppermute | solution.py:46
  158.8 2.7 %collective-permute-done.23 = f32[2,64,256]{2,1,0:T(8,128)S(1)} collective-permute-done((f32[2,64,256]{2,1,0:T(8,128)}, f32[2,64,256]{2,1,0:T(8,128)S(1)}, u32[]{:S(2)}, u32[]{:S(2)}) %collective-permute-start.23) | collective-permute-done | bytes 131104 | tf_op jit(solution)/shard_map/ppermute | solution.py:46
  162.7 2.9 %collective-permute-start.26 = (f32[64,256]{1,0:T(8,128)S(1)}, f32[64,256]{1,0:T(8,128)S(1)}, u32[]{:S(2)}, u32[]{:S(2)}) collective-permute-start(f32[64,256]{1,0:T(8,128)S(1)} %get-tuple-element.20), channel_id=1, source_target_pairs={{0,64},{1,65},{2,66},{3,67},{64,0},{65,1},{66,2},{67,3},{16,80},{1... | collective-permute-start | bytes 196616 | tf_op jit(solution)/shard_map/ppermute | solution.py:46
  166.1 2.1 %collective-permute-start.28 = (f32[128,1024]{1,0:T(8,128)}, f32[128,1024]{1,0:T(8,128)S(1)}, u32[]{:S(2)}, u32[]{:S(2)}) collective-permute-start(f32[128,1024]{1,0:T(8,128)} %get-tuple-element.17), channel_id=1, source_target_pairs={{0,2},{1,3},{2,0},{3,1},{64,66},{65,67},{66,64},{67,65},{16,18},{1... | collective-permute-start | bytes 1572872 | tf_op jit(solution)/shard_map/ppermute | solution.py:46
  168.5 1.4 collective-permute-done.27
  170.2 3.3 %collective-permute-start.31 = (f32[64,256]{1,0:T(8,128)S(1)}, f32[64,256]{1,0:T(8,128)S(1)}, u32[]{:S(2)}, u32[]{:S(2)}) collective-permute-start(f32[64,256]{1,0:T(8,128)S(1)} %add_add_fusion.1), channel_id=1, source_target_pairs={{0,32},{1,33},{2,34},{3,35},{64,96},{65,97},{66,98},{67,99},{16,48... | collective-permute-start | bytes 196616 | tf_op jit(solution)/shard_map/ppermute | solution.py:46
  173.5 1.9 %collective-permute-done.30 = f32[64,256]{1,0:T(8,128)S(1)} collective-permute-done((f32[64,256]{1,0:T(8,128)S(1)}, f32[64,256]{1,0:T(8,128)S(1)}, u32[]{:S(2)}, u32[]{:S(2)}) %collective-permute-start.30) | collective-permute-done | bytes 65568 | tf_op jit(solution)/shard_map/ppermute | solution.py:46
  178.5 3.8 %collective-permute-done.28 = f32[128,1024]{1,0:T(8,128)S(1)} collective-permute-done((f32[128,1024]{1,0:T(8,128)}, f32[128,1024]{1,0:T(8,128)S(1)}, u32[]{:S(2)}, u32[]{:S(2)}) %collective-permute-start.28) | collective-permute-done | bytes 524320 | tf_op jit(solution)/shard_map/ppermute | solution.py:46
  182.3 8.3 %collective-permute-done.29 = f32[128,1024]{1,0:T(8,128)S(1)} collective-permute-done((f32[128,1024]{1,0:T(8,128)}, f32[128,1024]{1,0:T(8,128)S(1)}, u32[]{:S(2)}, u32[]{:S(2)}) %collective-permute-start.29) | collective-permute-done | bytes 524320 | tf_op jit(solution)/shard_map/ppermute | solution.py:46
  (90 shorter events, 22.4 us)
Async XLA Ops:
  0.6 21.0 %collective-permute-start = (f32[256,1024]{1,0:T(8,128)}, f32[256,1024]{1,0:T(8,128)S(1)}, u32[]{:S(2)}, u32[]{:S(2)}) collective-permute-start(f32[256,1024]{1,0:T(8,128)} %bitcast.24), channel_id=1, source_target_pairs={{0,16},{1,49},{2,18},{3,51},{64,80},{65,113},{66,82},{67,115},{16,... | collective-permute-start | bytes 3145736 | tf_op jit(solution)/shard_map/ppermute | solution.py:46
  2.3 21.7 %collective-permute-start.4 = (f32[256,1024]{1,0:T(8,128)}, f32[256,1024]{1,0:T(8,128)S(1)}, u32[]{:S(2)}, u32[]{:S(2)}) collective-permute-start(f32[256,1024]{1,0:T(8,128)} %bitcast.25), channel_id=1, source_target_pairs={{0,64},{1,65},{64,0},{65,1},{18,82},{19,83},{82,18},{83,19},{32,96... | collective-permute-start | bytes 3145736 | tf_op jit(solution)/shard_map/ppermute | solution.py:46
  3.0 51.2 %collective-permute-start.14 = (f32[1024,512]{1,0:T(8,128)}, f32[1024,512]{1,0:T(8,128)}, u32[]{:S(2)}, u32[]{:S(2)}) collective-permute-start(f32[1024,512]{1,0:T(8,128)} %refs_14_.1), channel_id=1, source_target_pairs={{0,4},{1,13},{2,6},{3,15},{64,68},{65,77},{66,70},{67,79},{16,20},... | collective-permute-start | bytes 6291464 | tf_op jit(solution)/shard_map/ppermute | solution.py:46
  4.6 31.1 %collective-permute-start.2 = (f32[256,1024]{1,0:T(8,128)}, f32[256,1024]{1,0:T(8,128)S(1)}, u32[]{:S(2)}, u32[]{:S(2)}) collective-permute-start(f32[256,1024]{1,0:T(8,128)} %bitcast.26), channel_id=1, source_target_pairs={{0,48},{1,17},{2,50},{3,19},{64,112},{65,81},{66,114},{67,83},{16,... | collective-permute-start | bytes 3145736 | tf_op jit(solution)/shard_map/ppermute | solution.py:46
  10.4 45.3 %collective-permute-start.15 = (f32[1024,512]{1,0:T(8,128)}, f32[1024,512]{1,0:T(8,128)}, u32[]{:S(2)}, u32[]{:S(2)}) collective-permute-start(f32[1024,512]{1,0:T(8,128)} %refs_14_.1), channel_id=1, source_target_pairs={{0,12},{1,5},{2,14},{3,7},{64,76},{65,69},{66,78},{67,71},{16,28},... | collective-permute-start | bytes 6291464 | tf_op jit(solution)/shard_map/ppermute | solution.py:46
  22.6 13.1 %collective-permute-start.1 = (f32[128,1024]{1,0:T(8,128)S(1)}, f32[128,1024]{1,0:T(8,128)S(1)}, u32[]{:S(2)}, u32[]{:S(2)}) collective-permute-start(f32[128,1024]{1,0:T(8,128)S(1)} %slice.32), channel_id=1, source_target_pairs={{0,16},{1,49},{2,18},{3,51},{64,80},{65,113},{66,82},{67,115},{16,... | collective-permute-start | bytes 1572872 | tf_op jit(solution)/shard_map/ppermute | solution.py:46
  25.7 27.2 %collective-permute-start.6 = (f32[256,1024]{1,0:T(8,128)S(1)}, f32[256,1024]{1,0:T(8,128)S(1)}, u32[]{:S(2)}, u32[]{:S(2)}) collective-permute-start(f32[256,1024]{1,0:T(8,128)S(1)} %broadcast_select_fusion), channel_id=1, source_target_pairs={{0,16},{1,49},{2,64},{3,1},{64,80},{65,113},{66,0},{67,65},{16,18}... | collective-permute-start | bytes 3145736 | tf_op jit(solution)/shard_map/ppermute | solution.py:46
  35.6 52.3 %collective-permute-start.13 = (f32[1024,512]{1,0:T(8,128)S(1)}, f32[1024,512]{1,0:T(8,128)S(1)}, u32[]{:S(2)}, u32[]{:S(2)}) collective-permute-start(f32[1024,512]{1,0:T(8,128)S(1)} %copy-done.10), channel_id=1, source_target_pairs={{0,1},{1,0},{2,3},{3,2},{64,65},{65,64},{66,67},{67,66},{16,17},{1... | collective-permute-start | bytes 6291464 | tf_op jit(solution)/shard_map/ppermute | solution.py:46
  35.8 12.5 %collective-permute-start.3 = (f32[128,1024]{1,0:T(8,128)S(1)}, f32[128,1024]{1,0:T(8,128)S(1)}, u32[]{:S(2)}, u32[]{:S(2)}) collective-permute-start(f32[128,1024]{1,0:T(8,128)S(1)} %slice.33), channel_id=1, source_target_pairs={{0,48},{1,17},{2,50},{3,19},{64,112},{65,81},{66,114},{67,83},{16,... | collective-permute-start | bytes 1572872 | tf_op jit(solution)/shard_map/ppermute | solution.py:46
  48.3 18.4 %collective-permute-start.8 = (f32[256,1024]{1,0:T(8,128)S(1)}, f32[256,1024]{1,0:T(8,128)S(1)}, u32[]{:S(2)}, u32[]{:S(2)}) collective-permute-start(f32[256,1024]{1,0:T(8,128)S(1)} %broadcast_select_fusion), channel_id=1, source_target_pairs={{0,48},{1,17},{2,0},{3,65},{64,112},{65,81},{66,64},{67,1},{16,82}... | collective-permute-start | bytes 3145736 | tf_op jit(solution)/shard_map/ppermute | solution.py:46
  52.9 28.3 %collective-permute-start.10 = (f32[256,1024]{1,0:T(8,128)S(1)}, f32[256,1024]{1,0:T(8,128)S(1)}, u32[]{:S(2)}, u32[]{:S(2)}) collective-permute-start(f32[256,1024]{1,0:T(8,128)S(1)} %copy-done.7), channel_id=1, source_target_pairs={{0,66},{1,3},{64,2},{65,67},{18,16},{19,81},{82,80},{83,17},{32,98... | collective-permute-start | bytes 3145736 | tf_op jit(solution)/shard_map/ppermute | solution.py:46
  54.2 30.1 %collective-permute-start.5 = (f32[256,1024]{1,0:T(8,128)S(1)}, f32[256,1024]{1,0:T(8,128)S(1)}, u32[]{:S(2)}, u32[]{:S(2)}) collective-permute-start(f32[256,1024]{1,0:T(8,128)S(1)} %copy-done.7), channel_id=1, source_target_pairs={{0,2},{1,67},{64,66},{65,3},{18,80},{19,17},{82,16},{83,81},{32,34... | collective-permute-start | bytes 3145736 | tf_op jit(solution)/shard_map/ppermute | solution.py:46
  55.7 45.3 %collective-permute-start.11 = (f32[256,1024]{1,0:T(8,128)S(1)}, f32[256,1024]{1,0:T(8,128)S(1)}, u32[]{:S(2)}, u32[]{:S(2)}) collective-permute-start(f32[256,1024]{1,0:T(8,128)S(1)} %maximum_select_fusion), channel_id=1, source_target_pairs={{0,2},{1,67},{2,64},{3,1},{64,66},{65,3},{66,0},{67,65},{16,18},{1... | collective-permute-start | bytes 3145736 | tf_op jit(solution)/shard_map/ppermute | solution.py:46
  66.7 35.6 %collective-permute-start.12 = (f32[256,1024]{1,0:T(8,128)S(1)}, f32[256,1024]{1,0:T(8,128)S(1)}, u32[]{:S(2)}, u32[]{:S(2)}) collective-permute-start(f32[256,1024]{1,0:T(8,128)S(1)} %maximum_select_fusion), channel_id=1, source_target_pairs={{0,66},{1,3},{2,0},{3,65},{64,2},{65,67},{66,64},{67,1},{16,82},{1... | collective-permute-start | bytes 3145736 | tf_op jit(solution)/shard_map/ppermute | solution.py:46
  81.2 23.7 %collective-permute-start.18 = (f32[512,512]{1,0:T(8,128)S(1)}, f32[512,512]{1,0:T(8,128)}, u32[]{:S(2)}, u32[]{:S(2)}) collective-permute-start(f32[512,512]{1,0:T(8,128)S(1)} %slice.36), channel_id=1, source_target_pairs={{0,4},{1,13},{2,6},{3,15},{64,68},{65,77},{66,70},{67,79},{16,20},... | collective-permute-start | bytes 3145736 | tf_op jit(solution)/shard_map/ppermute | solution.py:46
  84.3 21.6 %collective-permute-start.19 = (f32[512,512]{1,0:T(8,128)S(1)}, f32[512,512]{1,0:T(8,128)}, u32[]{:S(2)}, u32[]{:S(2)}) collective-permute-start(f32[512,512]{1,0:T(8,128)S(1)} %slice.37), channel_id=1, source_target_pairs={{0,12},{1,5},{2,14},{3,7},{64,76},{65,69},{66,78},{67,71},{16,28},... | collective-permute-start | bytes 3145736 | tf_op jit(solution)/shard_map/ppermute | solution.py:46
  87.9 35.5 %collective-permute-start.16 = (f32[1024,512]{1,0:T(8,128)}, f32[1024,512]{1,0:T(8,128)S(1)}, u32[]{:S(2)}, u32[]{:S(2)}) collective-permute-start(f32[1024,512]{1,0:T(8,128)} %collective-permute-done.15.refs_18_), channel_id=1, source_target_pairs={{0,1},{1,0},{2,3},{3,2},{64,65},{65,64},{66,67},{67,66},{16,17},{1... | collective-permute-start | bytes 6291464 | tf_op jit(solution)/shard_map/ppermute | solution.py:46
  101.0 22.4 %collective-permute-start.17 = (f32[1024,512]{1,0:T(8,128)}, f32[1024,512]{1,0:T(8,128)}, u32[]{:S(2)}, u32[]{:S(2)}) collective-permute-start(f32[1024,512]{1,0:T(8,128)} %collective-permute-done.14.refs_16_), channel_id=1, source_target_pairs={{0,1},{1,0},{2,3},{3,2},{64,65},{65,64},{66,67},{67,66},{16,17},{1... | collective-permute-start | bytes 6291464 | tf_op jit(solution)/shard_map/ppermute | solution.py:46
  102.3 8.0 %collective-permute-start.7 = (f32[128,1024]{1,0:T(8,128)S(1)}, f32[128,1024]{1,0:T(8,128)S(1)}, u32[]{:S(2)}, u32[]{:S(2)}) collective-permute-start(f32[128,1024]{1,0:T(8,128)S(1)} %slice.34), channel_id=1, source_target_pairs={{2,18},{3,51},{66,82},{67,115},{16,32},{17,1},{80,96},{81,65},{34,... | collective-permute-start | bytes 1572872 | tf_op jit(solution)/shard_map/ppermute | solution.py:46
  104.9 18.4 %collective-permute-start.20 = (f32[512,512]{1,0:T(8,128)}, f32[512,512]{1,0:T(8,128)}, u32[]{:S(2)}, u32[]{:S(2)}) collective-permute-start(f32[512,512]{1,0:T(8,128)} %collective-permute-done.18.refs_20_), channel_id=1, source_target_pairs={{0,1},{1,0},{2,3},{3,2},{64,65},{65,64},{66,67},{67,66},{16,17},{1... | collective-permute-start | bytes 3145736 | tf_op jit(solution)/shard_map/ppermute | solution.py:46
  105.9 17.5 %collective-permute-start.21 = (f32[512,512]{1,0:T(8,128)}, f32[512,512]{1,0:T(8,128)}, u32[]{:S(2)}, u32[]{:S(2)}) collective-permute-start(f32[512,512]{1,0:T(8,128)} %collective-permute-done.19.refs_21_), channel_id=1, source_target_pairs={{0,1},{1,0},{2,3},{3,2},{64,65},{65,64},{66,67},{67,66},{16,17},{1... | collective-permute-start | bytes 3145736 | tf_op jit(solution)/shard_map/ppermute | solution.py:46
  110.3 13.1 %collective-permute-start.9 = (f32[128,1024]{1,0:T(8,128)S(1)}, f32[128,1024]{1,0:T(8,128)}, u32[]{:S(2)}, u32[]{:S(2)}) collective-permute-start(f32[128,1024]{1,0:T(8,128)S(1)} %slice.35), channel_id=1, source_target_pairs={{2,50},{3,19},{66,114},{67,83},{16,0},{17,33},{80,64},{81,97},{34,... | collective-permute-start | bytes 1572872 | tf_op jit(solution)/shard_map/ppermute | solution.py:46
  149.5 9.2 %collective-permute-start.22 = (f32[2,64,256]{2,1,0:T(8,128)}, f32[2,64,256]{2,1,0:T(8,128)S(1)}, u32[]{:S(2)}, u32[]{:S(2)}) collective-permute-start(f32[2,64,256]{2,1,0:T(8,128)} %get-tuple-element.13), channel_id=1, source_target_pairs={{0,16},{1,49},{2,18},{3,51},{64,80},{65,113},{66,82},{67,115},{16,... | collective-permute-start | bytes 393224 | tf_op jit(solution)/shard_map/ppermute | solution.py:46
  150.3 11.1 %collective-permute-start.23 = (f32[2,64,256]{2,1,0:T(8,128)}, f32[2,64,256]{2,1,0:T(8,128)S(1)}, u32[]{:S(2)}, u32[]{:S(2)}) collective-permute-start(f32[2,64,256]{2,1,0:T(8,128)} %get-tuple-element.14), channel_id=1, source_target_pairs={{0,32},{1,33},{2,34},{3,35},{64,96},{65,97},{66,98},{67,99},{16,48... | collective-permute-start | bytes 393224 | tf_op jit(solution)/shard_map/ppermute | solution.py:46
  154.8 6.7 %collective-permute-start.24 = (f32[2,64,256]{2,1,0:T(8,128)}, f32[2,64,256]{2,1,0:T(8,128)S(1)}, u32[]{:S(2)}, u32[]{:S(2)}) collective-permute-start(f32[2,64,256]{2,1,0:T(8,128)} %get-tuple-element.15), channel_id=1, source_target_pairs={{0,48},{1,17},{2,50},{3,19},{64,112},{65,81},{66,114},{67,83},{16,... | collective-permute-start | bytes 393224 | tf_op jit(solution)/shard_map/ppermute | solution.py:46
  162.4 5.8 %collective-permute-start.25 = (f32[64,256]{1,0:T(8,128)S(1)}, f32[64,256]{1,0:T(8,128)S(1)}, u32[]{:S(2)}, u32[]{:S(2)}) collective-permute-start(f32[64,256]{1,0:T(8,128)S(1)} %get-tuple-element.21), channel_id=1, source_target_pairs={{0,2},{1,3},{2,0},{3,1},{64,66},{65,67},{66,64},{67,65},{16,18},{1... | collective-permute-start | bytes 196616 | tf_op jit(solution)/shard_map/ppermute | solution.py:46
  162.7 5.8 %collective-permute-start.26 = (f32[64,256]{1,0:T(8,128)S(1)}, f32[64,256]{1,0:T(8,128)S(1)}, u32[]{:S(2)}, u32[]{:S(2)}) collective-permute-start(f32[64,256]{1,0:T(8,128)S(1)} %get-tuple-element.20), channel_id=1, source_target_pairs={{0,64},{1,65},{2,66},{3,67},{64,0},{65,1},{66,2},{67,3},{16,80},{1... | collective-permute-start | bytes 196616 | tf_op jit(solution)/shard_map/ppermute | solution.py:46
  165.6 4.3 %collective-permute-start.27 = (f32[64,256]{1,0:T(8,128)S(1)}, f32[64,256]{1,0:T(8,128)S(1)}, u32[]{:S(2)}, u32[]{:S(2)}) collective-permute-start(f32[64,256]{1,0:T(8,128)S(1)} %get-tuple-element.21), channel_id=1, source_target_pairs={{0,66},{1,67},{2,64},{3,65},{64,2},{65,3},{66,0},{67,1},{16,82},{1... | collective-permute-start | bytes 196616 | tf_op jit(solution)/shard_map/ppermute | solution.py:46
  166.1 16.2 %collective-permute-start.28 = (f32[128,1024]{1,0:T(8,128)}, f32[128,1024]{1,0:T(8,128)S(1)}, u32[]{:S(2)}, u32[]{:S(2)}) collective-permute-start(f32[128,1024]{1,0:T(8,128)} %get-tuple-element.17), channel_id=1, source_target_pairs={{0,2},{1,3},{2,0},{3,1},{64,66},{65,67},{66,64},{67,65},{16,18},{1... | collective-permute-start | bytes 1572872 | tf_op jit(solution)/shard_map/ppermute | solution.py:46
  168.1 22.5 %collective-permute-start.29 = (f32[128,1024]{1,0:T(8,128)}, f32[128,1024]{1,0:T(8,128)S(1)}, u32[]{:S(2)}, u32[]{:S(2)}) collective-permute-start(f32[128,1024]{1,0:T(8,128)} %get-tuple-element.18), channel_id=1, source_target_pairs={{0,2},{1,3},{2,0},{3,1},{64,66},{65,67},{66,64},{67,65},{16,18},{1... | collective-permute-start | bytes 1572872 | tf_op jit(solution)/shard_map/ppermute | solution.py:46
  169.9 5.5 %collective-permute-start.30 = (f32[64,256]{1,0:T(8,128)S(1)}, f32[64,256]{1,0:T(8,128)S(1)}, u32[]{:S(2)}, u32[]{:S(2)}) collective-permute-start(f32[64,256]{1,0:T(8,128)S(1)} %add_add_fusion.1), channel_id=1, source_target_pairs={{0,16},{1,49},{2,18},{3,51},{64,80},{65,113},{66,82},{67,115},{16,... | collective-permute-start | bytes 196616 | tf_op jit(solution)/shard_map/ppermute | solution.py:46
  170.2 6.2 %collective-permute-start.31 = (f32[64,256]{1,0:T(8,128)S(1)}, f32[64,256]{1,0:T(8,128)S(1)}, u32[]{:S(2)}, u32[]{:S(2)}) collective-permute-start(f32[64,256]{1,0:T(8,128)S(1)} %add_add_fusion.1), channel_id=1, source_target_pairs={{0,32},{1,33},{2,34},{3,35},{64,96},{65,97},{66,98},{67,99},{16,48... | collective-permute-start | bytes 196616 | tf_op jit(solution)/shard_map/ppermute | solution.py:46
  (19 other events, 399.6 us)
